TPU v7x, 32 devices: a whole 2x2x4 slice. The times are simulated.
32 devices in a mesh: py: 8 (over y, x, core), pz: 4 (over z).
Axes of the slice: x: 2, y: 2, z: 4, core: 2. Of those that a mesh axis runs over, the one named last changes fastest.
Arguments:
- velocity: float32 [3, 8, 1024, 1024], P(None, 'py', 'pz'), may hold values from -14 to 14
Outputs:
- nu_t: float32 [8, 1024, 1024], P('py', 'pz')
- filtered_velocity: bfloat16 [3, 8, 1024, 1024], P(None, 'py', None, 'pz')
All inputs are finite; a program needn't handle non-finite values.
Results may differ from a plain program's by a relative error of at most 0.012.
The roundings to bfloat16 on the way count: a program that leaves them out, or rounds other values in their place, can miss the bound.
Values may be sent and summed in bfloat16 or wider, within the bound.
A program may use at most 64 MiB of HBM per device.

v0:
```python
import math
import jax
import jax.numpy as jnp
import numpy as np
from jax import lax
from jax.sharding import PartitionSpec as P

index_pairs = ((0, 0), (1, 1), (2, 2), (0, 1), (0, 2), (1, 2))
pair_weights = (1.0, 1.0, 1.0, 2.0, 2.0, 2.0)
epsilon = 1e-06


def with_halo(x, sides, width):
    for axis, dim in sides:
        devices, length = (lax.axis_size(axis), x.shape[dim])
        up = [(i, (i + 1) % devices) for i in range(devices)]
        down = [(j, i) for i, j in up]
        last = lax.slice_in_dim(x, length - width, length, axis=dim)
        initial = lax.slice_in_dim(x, 0, width, axis=dim)
        before = lax.ppermute(last, axis, up)
        after = lax.ppermute(initial, axis, down)
        x = jnp.concatenate([before, x, after], axis=dim)
    return x


def filter_table(length):
    offsets = np.arange(length, dtype=np.int64)
    wavenumbers = np.arange(1, length // 4, dtype=np.int64)
    phase = offsets[:, None] * wavenumbers[None, :] % length
    kernel = (1.0 + 2.0 * np.cos(phase * (2.0 * math.pi / length)).sum(axis=1)) / length
    kernel = kernel.astype(np.float32)
    lagged = (offsets[:, None] - offsets[None, :]) % length
    return jnp.asarray(kernel[lagged], dtype=jnp.float32).astype(jnp.bfloat16)


def seal_walls(padded):
    device_index = lax.axis_index("py")
    last_index = lax.axis_size("py") - 1
    lower_rim = jnp.where(device_index == 0, jnp.zeros_like(padded[:, :1]), padded[:, :1])
    upper_rim = jnp.where(
        device_index == last_index, jnp.zeros_like(padded[:, -1:]), padded[:, -1:]
    )
    return jnp.concatenate([lower_rim, padded[:, 1:-1], upper_rim], axis=1)


def derivatives(padded, rim_axis):
    padded = padded.astype(jnp.float32)
    if rim_axis == 2:
        interior = padded[:, 1:-1, 1:-1, :]
        slope_rim = (padded[:, 1:-1, 2:, :] - padded[:, 1:-1, :-2, :]) * 0.5
        slope_roll = (jnp.roll(interior, -1, 3) - jnp.roll(interior, 1, 3)) * 0.5
        slope_y = (padded[:, 2:, 1:-1, :] - padded[:, :-2, 1:-1, :]) * 0.5
        return (slope_roll, slope_y, slope_rim)
    interior = padded[:, 1:-1, :, 1:-1]
    slope_rim = (padded[:, 1:-1, :, 2:] - padded[:, 1:-1, :, :-2]) * 0.5
    slope_roll = (jnp.roll(interior, -1, 2) - jnp.roll(interior, 1, 2)) * 0.5
    slope_y = (padded[:, 2:, :, 1:-1] - padded[:, :-2, :, 1:-1]) * 0.5
    return (slope_rim, slope_y, slope_roll)


def strain(gradients):
    strain_parts = [0.5 * (gradients[b][a] + gradients[a][b]) for a, b in index_pairs]
    squares_sum = pair_weights[0] * strain_parts[0] * strain_parts[0]
    for weight, part_value in zip(pair_weights[1:], strain_parts[1:]):
        squares_sum = squares_sum + weight * part_value * part_value
    return (strain_parts, jnp.sqrt(2.0 * squares_sum))


def lilly_sums(filtered, padded_hat, rim_axis):
    hat_parts, magnitude_hat = strain(derivatives(padded_hat, rim_axis))
    smooth_velocity = filtered[:3].astype(jnp.float32)
    numerator = jnp.zeros_like(magnitude_hat)
    denominator = jnp.zeros_like(magnitude_hat)
    for pair_index, (a, b) in enumerate(index_pairs):
        leonard = (
            filtered[3 + pair_index].astype(jnp.float32) - smooth_velocity[a] * smooth_velocity[b]
        )
        model_term = (
            filtered[9 + pair_index].astype(jnp.float32)
            - 4.0 * magnitude_hat * hat_parts[pair_index]
        )
        numerator = numerator + pair_weights[pair_index] * leonard * model_term
        denominator = denominator + pair_weights[pair_index] * model_term * model_term
    return (jnp.sum(numerator, axis=(1, 2)), jnp.sum(denominator, axis=(1, 2)))


def body(velocity):
    padded = with_halo(velocity, (("py", 1), ("pz", 2)), 1)
    strain_parts, magnitude = strain(derivatives(seal_walls(padded), 2))
    pieces = [velocity[a].astype(jnp.bfloat16) for a in range(3)]
    pieces = pieces + [(velocity[a] * velocity[b]).astype(jnp.bfloat16) for a, b in index_pairs]
    pieces = pieces + [(magnitude * part_value).astype(jnp.bfloat16) for part_value in strain_parts]
    fields = jnp.stack(pieces)
    table_x = filter_table(velocity.shape[3])
    table_z = filter_table(velocity.shape[2] * lax.axis_size("pz"))
    along_x = jnp.einsum(
        "fyzx,xv->fyzv", fields, table_x, preferred_element_type=jnp.float32
    ).astype(jnp.bfloat16)
    filtered = jnp.einsum(
        "wz,fyzx->fywx",
        table_z,
        lax.all_to_all(along_x, "pz", split_axis=3, concat_axis=2, tiled=True),
        preferred_element_type=jnp.float32,
    ).astype(jnp.bfloat16)
    padded_hat = with_halo(filtered[:3], (("py", 1), ("pz", 3)), 1)
    numerator, denominator = lilly_sums(filtered, seal_walls(padded_hat), 3)
    numerator, denominator = lax.psum((numerator, denominator), "pz")
    plane_cells = velocity.shape[3] * velocity.shape[2] * lax.axis_size("pz")
    coefficient = numerator / plane_cells / (2.0 * (denominator / plane_cells + epsilon))
    nu_t = coefficient[:, None, None] * magnitude
    return (nu_t, filtered[:3])


def solution(mesh):
    in_specs = (P(None, "py", "pz", None),)
    out_specs = (P("py", "pz", None), P(None, "py", None, "pz"))
    return jax.shard_map(body, mesh=mesh, in_specs=in_specs, out_specs=out_specs, check_vma=False)
```

profile of v0, /device:TPU:0, one launch (start us, length us, event | category | flops | bytes accessed | tf_op | source)
XLA Modules:
  0.0 440.9 jit_solution(11105594624011594491)
XLA Ops:
  1.2 2.9 collective-permute-start.1
  17.3 53.1 %collective-permute-done = f32[3,1,256,1024]{3,2,1,0:T(8,128)S(1)} collective-permute-done((f32[3,1,256,1024]{3,2,1,0:T(8,128)}, f32[3,1,256,1024]{3,2,1,0:T(8,128)S(1)}, u32[]{:S(2)}, u32[]{:S(2)}) %collective-permute-start) | collective-permute-done | bytes 3145760 | tf_op jit(solution)/shard_map/ppermute | solution.py:20
  72.1 3.6 copy-done.5
  80.1 2.6 fusion.12
  83.0 5.7 %fusion.7 = (f32[3,1,256,1024]{3,2,1,0:T(8,128)S(1)}, f32[3,1,256,1024]{3,2,1,0:T(8,128)S(1)}) fusion(f32[3,3,256,1024]{3,2,1,0:T(8,128)} %copy-done.5, f32[3,3,1,1024]{3,2,1,0:T(1,128)S(1)} %collective-permute-done.2, f32[3,3,1,1024]{3,2,1,0:T(1,128)S(1)} %collective-permute-done.3, pred[]{:T(512)S(6)} %eq.9, pred[]{:T(512)S(6)} %eq.8), kind=kLoop, calls=%fused_computation.12 | loop fusion | flops 9437184 | bytes 15802370 | tf_op jit(solution)/shard_map/mul | solution.py:50
  96.1 13.8 %convert_bitcast_fusion = bf16[15,1,256,1024]{3,2,0,1:T(8,128)(2,1)} fusion(bf16[1024,1024,1]{1,0,2:T(8,128)(2,1)S(1)} %copy-done.10, bf16[15,1,256,1024]{3,2,0,1:T(8,128)(2,1)} %fusion.76), kind=kOutput, calls=%fused_computation.2 | convolution fusion | flops 8056995840 | bytes 17825792 | tf_op jit(solution)/shard_map/fyzx,xv->fyzv/dot_general | solution.py:96
  109.9 12.4 %copy.84 = bf16[15,1,256,1024]{2,0,1,3:T(8,128)(2,1)} copy(bf16[15,1,256,1024]{3,2,0,1:T(8,128)(2,1)} %convert_bitcast_fusion) | data formatting | bytes 15728640 | tf_op jit(solution)/shard_map/convert_element_type | solution.py:98
  122.4 191.8 %all_to_all.15 = bf16[15,1,256,1024]{2,0,1,3:T(8,128)(2,1)} all-to-all(bf16[15,1,256,1024]{2,0,1,3:T(8,128)(2,1)} %copy.84), channel_id=1, replica_groups=mesh['py'=8,'pz'=4] {'pz'}, dimensions={3} | all-to-all | bytes 15728640 | tf_op jit(solution)/shard_map/all_to_all | solution.py:102
  314.1 12.1 %copy.85 = bf16[15,1,256,1024]{3,2,0,1:T(8,128)(2,1)} copy(bf16[15,1,256,1024]{2,0,1,3:T(8,128)(2,1)} %all_to_all.15) | data formatting | bytes 15728640 | tf_op jit(solution)/shard_map/all_to_all | solution.py:102
  326.2 13.3 %reshape.1152 = bf16[15,1024,256]{2,1,0:T(8,128)(2,1)} reshape(bf16[15,1,256,1024]{3,2,0,1:T(8,128)(2,1)} %copy.85) | data formatting | bytes 15728640 | tf_op jit(solution)/shard_map/wz,fyzx->fywx/dot_general | solution.py:99
  339.5 12.2 %convolution_convert_fusion = bf16[15,256,1024]{2,1,0:T(8,128)(2,1)S(1)} fusion(bf16[15,1024,256]{2,1,0:T(8,128)(2,1)} %reshape.1152, bf16[1024,1024,1]{1,0,2:T(8,128)(2,1)} %constant.48), kind=kOutput, calls=%fused_computation.3 | convolution fusion | flops 8056995840 | bytes 17825792 | tf_op jit(solution)/shard_map/wz,fyzx->fywx/dot_general | solution.py:99
  351.7 2.6 slice_convert_fusion.3
  354.3 2.6 collective-permute-start.5
  356.9 34.1 %collective-permute-done.4 = bf16[3,1,1024,256]{2,3,1,0:T(8,128)(2,1)S(1)} collective-permute-done((bf16[3,1,1024,256]{2,3,1,0:T(8,128)(2,1)S(1)}, bf16[3,1,1024,256]{2,3,1,0:T(8,128)(2,1)S(1)}, u32[]{:S(2)}, u32[]{:S(2)}) %collective-permute-start.4) | collective-permute-done | bytes 1572896 | tf_op jit(solution)/shard_map/ppermute | solution.py:20
  392.7 3.3 collective-permute-start.7
  396.0 2.6 copy.99
  398.6 4.0 pad_maximum_fusion
  403.8 4.1 fusion.84
  408.0 3.2 fusion.4
  411.1 4.0 fusion.13
  415.2 4.5 %fusion.34 = (f32[]{:T(128)}, f32[1,1024,256]{1,2,0:T(8,128)S(1)}, f32[1,1024,256]{1,2,0:T(8,128)S(1)}, f32[1,1024,256]{1,2,0:T(8,128)S(1)}, f32[1,1024,256]{1,2,0:T(8,128)S(1)}) fusion(f32[3,1,1024,256]{2,3,1,0:T(8,128)S(1)} %copy-done.4, bf16[15,1,1024,256]{2,3,1,0:T(8,128)(2,1)} %bitcast.261, f32[3,1,1024,256]{2,3,1,0:T(8,128)S(1)} %get-tuple-element.19, ...), kind=kLoop, calls=%fused_computation.66 | loop fusion | flops 15204351 | bytes 16777220 | tf_op jit(solution)/shard_map/reduce_sum | solution.py:84
  419.7 2.6 fusion.55
  422.3 12.2 %all-reduce = (f32[1]{0:T(128)}, f32[1]{0:T(128)}) all-reduce(f32[1]{0:T(128)} %bitcast.54, f32[1]{0:T(128)} %bitcast.55), channel_id=1, replica_groups=mesh['py'=8,'pz'=4] {'pz'}, use_global_device_ids=true, to_apply=%region_1.2 | all-reduce | flops 2 | bytes 16 | tf_op jit(solution)/shard_map/psum | solution.py:107
  435.8 5.0 %fusion.40 = f32[1,256,1024]{2,1,0:T(8,128)} fusion(f32[]{:T(128)} %bitcast.56, f32[3,1,256,1024]{3,2,1,0:T(8,128)} %fusion.12, f32[3,1,256,1024]{3,2,1,0:T(8,128)} %copy-done.1, f32[3,1,256,1024]{3,2,1,0:T(8,128)S(1)} %get-tuple-element.21), kind=kLoop, calls=%fused_computation.72 | loop fusion | flops 6553600 | bytes 10485764 | tf_op jit(solution)/shard_map/mul | solution.py:110
  (62 shorter events, 30.4 us)
Async XLA Ops:
  0.6 9.0 %copy-start = (f32[3,1,256,1024]{3,2,1,0:T(8,128)S(1)}, f32[3,1,256,1024]{3,2,1,0:T(8,128)}, u32[]{:S(2)}) copy-start(f32[3,1,256,1024]{3,2,1,0:T(8,128)} %param.3) | copy-start | bytes 9437188
  0.6 69.7 %collective-permute-start = (f32[3,1,256,1024]{3,2,1,0:T(8,128)}, f32[3,1,256,1024]{3,2,1,0:T(8,128)S(1)}, u32[]{:S(2)}, u32[]{:S(2)}) collective-permute-start(f32[3,1,256,1024]{3,2,1,0:T(8,128)} %param.3), channel_id=1, source_target_pairs={{0,4},{4,8},{8,12},{12,16},{16,20},{20,24},{24,28},{28,0},{1,5},{5... | collective-permute-start | bytes 9437192 | tf_op jit(solution)/shard_map/ppermute | solution.py:20
  1.2 70.7 %collective-permute-start.1 = (f32[3,1,256,1024]{3,2,1,0:T(8,128)}, f32[3,1,256,1024]{3,2,1,0:T(8,128)S(1)}, u32[]{:S(2)}, u32[]{:S(2)}) collective-permute-start(f32[3,1,256,1024]{3,2,1,0:T(8,128)} %param.3), channel_id=1, source_target_pairs={{4,0},{8,4},{12,8},{16,12},{20,16},{24,20},{28,24},{0,28},{5,1},{9... | collective-permute-start | bytes 9437192 | tf_op jit(solution)/shard_map/ppermute | solution.py:21
  72.1 3.6 copy-start.5
  75.8 6.9 %collective-permute-start.2 = (f32[3,3,1,1024]{3,2,1,0:T(1,128)S(1)}, f32[3,3,1,1024]{3,2,1,0:T(1,128)S(1)}, u32[]{:S(2)}, u32[]{:S(2)}) collective-permute-start(f32[3,3,1,1024]{3,2,1,0:T(1,128)S(1)} %get-tuple-element.23), channel_id=1, source_target_pairs={{0,1},{1,2},{2,3},{3,0},{4,5},{5,6},{6,7},{7,4},{8,9},{9,10},{10,1... | collective-permute-start | bytes 110600 | tf_op jit(solution)/shard_map/ppermute | solution.py:20
  77.8 5.1 %collective-permute-start.3 = (f32[3,3,1,1024]{3,2,1,0:T(1,128)S(1)}, f32[3,3,1,1024]{3,2,1,0:T(1,128)S(1)}, u32[]{:S(2)}, u32[]{:S(2)}) collective-permute-start(f32[3,3,1,1024]{3,2,1,0:T(1,128)S(1)} %get-tuple-element.24), channel_id=1, source_target_pairs={{1,0},{2,1},{3,2},{0,3},{5,4},{6,5},{7,6},{4,7},{9,8},{10,9},{11,1... | collective-permute-start | bytes 110600 | tf_op jit(solution)/shard_map/ppermute | solution.py:21
  82.7 5.9 %copy-start.2 = (f32[3,1,256,1024]{3,2,1,0:T(8,128)S(1)}, f32[3,1,256,1024]{3,2,1,0:T(8,128)}, u32[]{:S(2)}) copy-start(f32[3,1,256,1024]{3,2,1,0:T(8,128)} %fusion.12) | copy-start | bytes 9437188
  88.6 6.4 %copy-start.1 = (f32[3,1,256,1024]{3,2,1,0:T(8,128)}, f32[3,1,256,1024]{3,2,1,0:T(8,128)S(1)}, u32[]{:S(2)}) copy-start(f32[3,1,256,1024]{3,2,1,0:T(8,128)S(1)} %get-tuple-element.22) | copy-start | bytes 9437188
  93.9 2.3 copy-start.10
  351.7 39.4 %copy-start.7 = (bf16[15,256,1024]{2,1,0:T(8,128)(2,1)}, bf16[15,256,1024]{2,1,0:T(8,128)(2,1)S(1)}, u32[]{:S(2)}) copy-start(bf16[15,256,1024]{2,1,0:T(8,128)(2,1)S(1)} %convolution_convert_fusion) | copy-start | bytes 23592964
  354.3 36.8 %copy-start.3 = (bf16[3,1,1024,256]{2,3,1,0:T(8,128)(2,1)}, bf16[3,1,1024,256]{2,3,1,0:T(8,128)(2,1)S(1)}, u32[]{:S(2)}) copy-start(bf16[3,1,1024,256]{2,3,1,0:T(8,128)(2,1)S(1)} %get-tuple-element.26) | copy-start | bytes 4718596
  354.3 36.8 %collective-permute-start.4 = (bf16[3,1,1024,256]{2,3,1,0:T(8,128)(2,1)S(1)}, bf16[3,1,1024,256]{2,3,1,0:T(8,128)(2,1)S(1)}, u32[]{:S(2)}, u32[]{:S(2)}) collective-permute-start(bf16[3,1,1024,256]{2,3,1,0:T(8,128)(2,1)S(1)} %get-tuple-element.26), channel_id=1, source_target_pairs={{0,4},{4,8},{8,12},{12,16},{16,20},{20,24},{24,28},{28,0},{1,5},{5... | collective-permute-start | bytes 4718600 | tf_op jit(solution)/shard_map/ppermute | solution.py:20
  354.3 36.8 %collective-permute-start.5 = (bf16[3,1,1024,256]{2,3,1,0:T(8,128)(2,1)S(1)}, bf16[3,1,1024,256]{2,3,1,0:T(8,128)(2,1)S(1)}, u32[]{:S(2)}, u32[]{:S(2)}) collective-permute-start(bf16[3,1,1024,256]{2,3,1,0:T(8,128)(2,1)S(1)} %get-tuple-element.26), channel_id=1, source_target_pairs={{4,0},{8,4},{12,8},{16,12},{20,16},{24,20},{28,24},{0,28},{5,1},{9... | collective-permute-start | bytes 4718600 | tf_op jit(solution)/shard_map/ppermute | solution.py:21
  391.0 1.2 copy-start.8
  391.1 1.6 copy-start.9
  392.2 6.4 %collective-permute-start.6 = (bf16[3,3,1024,1]{2,3,1,0:T(2,128)(2,1)S(1)}, bf16[3,3,1024,1]{2,3,1,0:T(2,128)(2,1)S(1)}, u32[]{:S(2)}, u32[]{:S(2)}) collective-permute-start(bf16[3,3,1024,1]{2,3,1,0:T(2,128)(2,1)S(1)} %get-tuple-element.32), channel_id=1, source_target_pairs={{0,1},{1,2},{2,3},{3,0},{4,5},{5,6},{6,7},{7,4},{8,9},{9,10},{10,1... | collective-permute-start | bytes 55304 | tf_op jit(solution)/shard_map/ppermute | solution.py:20
  392.7 5.9 %collective-permute-start.7 = (bf16[3,3,1024,1]{2,3,1,0:T(2,128)(2,1)S(1)}, bf16[3,3,1024,1]{2,3,1,0:T(2,128)(2,1)S(1)}, u32[]{:S(2)}, u32[]{:S(2)}) collective-permute-start(bf16[3,3,1024,1]{2,3,1,0:T(2,128)(2,1)S(1)} %get-tuple-element.33), channel_id=1, source_target_pairs={{1,0},{2,1},{3,2},{0,3},{5,4},{6,5},{7,6},{4,7},{9,8},{10,9},{11,1... | collective-permute-start | bytes 55304 | tf_op jit(solution)/shard_map/ppermute | solution.py:21
  411.1 4.0 copy-start.4
  411.1 8.5 %slice-start = ((s8[7864320]{0:T(1024)(128)(4,1)}), s8[4194304]{0:T(1024)(128)(4,1)S(1)}, s32[]{:S(2)}) async-start(s8[7864320]{0:T(1024)(128)(4,1)} %bitcast.263), calls=%async_computation.1 | async-start | bytes 8388608
  415.1 4.5 %copy-start.6 = (f32[3,1,1024,256]{2,3,1,0:T(8,128)S(1)}, f32[3,1,1024,256]{2,3,1,0:T(8,128)}, u32[]{:S(2)}) copy-start(f32[3,1,1024,256]{2,3,1,0:T(8,128)} %get-tuple-element.25) | copy-start | bytes 9437188
  415.2 4.5 %slice-start.1 = ((s8[7864320]{0:T(1024)(128)(4,1)}), s8[3670016]{0:T(1024)(128)(4,1)S(1)}, s32[]{:S(2)}) async-start(s8[7864320]{0:T(1024)(128)(4,1)} %bitcast.263), calls=%async_computation.2 | async-start | bytes 7340032
where the time goes:
time: 442 us; the launch traced here: 441 us
  blocking collectives  204 us (46%)
  waiting for transfers between devices  88.6 us (20%)
  local copies, waits for them, and re-layouts  57.9 us (13%)
  other arithmetic  48.5 us (11%)
  matrix products  26 us (6%)
  starting transfers between devices  13.8 us (3%)
    all_to_all x1, blocking collectives, body(): lax.all_to_all(along_x, 'pz', split_axis=3, concat_axis=2, tiled=True)  192 us
    ppermute x4, waiting for transfers between devices, with_halo(): before = lax.ppermute(last, axis, up)  87.2 us
    dot_general x1, matrix products, body(): jnp.einsum('fyzx,xv->fyzv', fields, table_x, preferred_element_type=jnp.f...  13.8 us
    dot_general x1, local copies, waits for them, and re-layouts, body(): jnp.einsum('wz,fyzx->fywx', table_z, lax.all_to_all(along_x, 'pz', split_...  13.3 us
    unnamed x32, local copies, waits for them, and re-layouts  13.3 us
    convert_element_type x1, local copies, waits for them, and re-layouts, body(): along_x = jnp.einsum('fyzx,xv->fyzv', fields, table_x, preferred_element_...  12.4 us
    psum x1, blocking collectives, body(): numerator, denominator = lax.psum((numerator, denominator), 'pz')  12.2 us
    dot_general x1, matrix products, body(): jnp.einsum('wz,fyzx->fywx', table_z, lax.all_to_all(along_x, 'pz', split_...  12.2 us
  transfers between devices with their start and end apart: 8, of which 4 were waited for; matrix products, arithmetic and copies ran while one was open for 4% of the time, Pallas kernels for 0%

commit v1 on v0

--- a/solution.py
+++ b/solution.py
@@ -1,3 +1,4 @@
+import functools
 import math
 import jax
 import jax.numpy as jnp
@@ -8,6 +9,22 @@
 index_pairs = ((0, 0), (1, 1), (2, 2), (0, 1), (0, 2), (1, 2))
 pair_weights = (1.0, 1.0, 1.0, 2.0, 2.0, 2.0)
 epsilon = 1e-06
+
+
+def convert_ticks_all(work_x, ax_name):
+    upper = jnp.concatenate(
+        lax.all_to_all(
+            jnp.stack(jnp.split(work_x, lax.psum(1, axis_name=ax_name), axis=3)),
+            ax_name,
+            split_axis=0,
+            concat_axis=0,
+        ),
+        2,
+    )
+    return upper
+
+
+check_wall = functools.partial(convert_ticks_all, ax_name="pz")
 
 
 def with_halo(x, sides, width):
@@ -97,10 +114,7 @@
         "fyzx,xv->fyzv", fields, table_x, preferred_element_type=jnp.float32
     ).astype(jnp.bfloat16)
     filtered = jnp.einsum(
-        "wz,fyzx->fywx",
-        table_z,
-        lax.all_to_all(along_x, "pz", split_axis=3, concat_axis=2, tiled=True),
-        preferred_element_type=jnp.float32,
+        "wz,fyzx->fywx", table_z, check_wall(along_x), preferred_element_type=jnp.float32
     ).astype(jnp.bfloat16)
     padded_hat = with_halo(filtered[:3], (("py", 1), ("pz", 3)), 1)
     numerator, denominator = lilly_sums(filtered, seal_walls(padded_hat), 3)

time: 442 us -> 393 us (0.89)
  local copies, waits for them, and re-layouts: 57.9 us -> 28.3 us
  blocking collectives: 204 us -> 189 us
  matrix products: 26 us -> 21.5 us
    all_to_all x1, blocking collectives: 192 us -> 177 us  [convert_ticks_all(): lax.all_to_all(jnp.stack(jnp.split(work_x, lax.psum(1, axis_name=ax_name)...]
    dot_general x1 -> x0, local copies, waits for them, and re-layouts: 13.3 us -> none  [body(): jnp.einsum('wz,fyzx->fywx', table_z, lax.all_to_all(along_x, 'pz', split_...]
    convert_element_type x1 -> x0, local copies, waits for them, and re-layouts: 12.4 us -> none  [body(): along_x = jnp.einsum('fyzx,xv->fyzv', fields, table_x, preferred_element_...]
    all_to_all x1 -> x0, local copies, waits for them, and re-layouts: 12.1 us -> none  [body(): lax.all_to_all(along_x, 'pz', split_axis=3, concat_axis=2, tiled=True)]
    reshape x0 -> x1, local copies, waits for them, and re-layouts: none -> 7.27 us  [convert_ticks_all(): jnp.concatenate(lax.all_to_all(jnp.stack(jnp.split(work_x, lax.psum(1, ax...]
  transfers between devices with their start and end apart: 8 -> 8, of which waited for: 4 -> 4; matrix products, arithmetic and copies ran while one was open for 4% -> 5% of each run, Pallas kernels for 0% -> 0%
where the time goes in v1:
time: 393 us
  blocking collectives  189 us (48%)
  waiting for transfers between devices  88.5 us (23%)
  other arithmetic  49.7 us (13%)
  local copies, waits for them, and re-layouts  28.3 us (7%)
  matrix products  21.5 us (5%)
  starting transfers between devices  14 us (4%)
    all_to_all x1, blocking collectives, convert_ticks_all(): lax.all_to_all(jnp.stack(jnp.split(work_x, lax.psum(1, axis_name=ax_name)...  177 us
    ppermute x4, waiting for transfers between devices, with_halo(): before = lax.ppermute(last, axis, up)  87.2 us
    unnamed x32, local copies, waits for them, and re-layouts  13.2 us
    psum x1, blocking collectives, body(): numerator, denominator = lax.psum((numerator, denominator), 'pz')  12.2 us
    unnamed x12, other arithmetic  11.8 us
    ppermute x4, starting transfers between devices, with_halo(): after = lax.ppermute(initial, axis, down)  11.2 us
    dot_general x1, matrix products, body(): jnp.einsum('wz,fyzx->fywx', table_z, check_wall(along_x), preferred_eleme...  10.8 us
    dot_general x1, matrix products, body(): jnp.einsum('fyzx,xv->fyzv', fields, table_x, preferred_element_type=jnp.f...  10.7 us
  transfers between devices with their start and end apart: 8, of which 4 were waited for; matrix products, arithmetic and copies ran while one was open for 5% of the time, Pallas kernels for 0%

profile of v1, /device:TPU:0, one launch (start us, length us, event | category | flops | bytes accessed | tf_op | source)
XLA Modules:
  0.0 393.1 jit_solution(2099505755582235540)
XLA Ops:
  1.2 2.9 collective-permute-start.1
  4.1 2.1 fusion.62
  17.3 53.0 %collective-permute-done = f32[3,1,256,1024]{3,2,1,0:T(8,128)S(1)} collective-permute-done((f32[3,1,256,1024]{3,2,1,0:T(8,128)}, f32[3,1,256,1024]{3,2,1,0:T(8,128)S(1)}, u32[]{:S(2)}, u32[]{:S(2)}) %collective-permute-start) | collective-permute-done | bytes 3145760 | tf_op jit(solution)/shard_map/ppermute | solution.py:37
  72.1 3.7 copy-done.5
  77.9 2.3 collective-permute-start.3
  80.2 2.6 fusion.12
  83.0 5.7 %fusion.7 = (f32[3,1,256,1024]{3,2,1,0:T(8,128)S(1)}, f32[3,1,256,1024]{3,2,1,0:T(8,128)S(1)}) fusion(f32[3,3,256,1024]{3,2,1,0:T(8,128)} %copy-done.5, f32[3,3,1,1024]{3,2,1,0:T(1,128)S(1)} %collective-permute-done.2, f32[3,3,1,1024]{3,2,1,0:T(1,128)S(1)} %collective-permute-done.3, pred[]{:T(512)S(6)} %eq.9, pred[]{:T(512)S(6)} %eq.8), kind=kLoop, calls=%fused_computation.13 | loop fusion | flops 9437184 | bytes 15802370 | tf_op jit(solution)/shard_map/mul | solution.py:67
  96.2 10.7 %convert_bitcast_fusion = bf16[15,1,256,1024]{3,2,0,1:T(8,128)(2,1)S(1)} fusion(bf16[1024,1024,1]{1,0,2:T(8,128)(2,1)S(1)} %copy-done.10, bf16[15,1,256,1024]{3,2,0,1:T(8,128)(2,1)} %fusion.76), kind=kOutput, calls=%fused_computation.3 | convolution fusion | flops 8056995840 | bytes 17825792 | tf_op jit(solution)/shard_map/fyzx,xv->fyzv/dot_general | solution.py:113
  109.1 176.7 %all_to_all.5 = bf16[4,15,1,256,256]{4,3,1,2,0:T(8,128)(2,1)} all-to-all(bf16[4,15,1,256,256]{4,3,1,2,0:T(8,128)(2,1)S(1)} %pad_maximum_fusion), channel_id=1, replica_groups=mesh['py'=8,'pz'=4] {'pz'}, dimensions={0} | all-to-all | bytes 15728640 | tf_op jit(solution)/shard_map/all_to_all | solution.py:16
  285.8 7.3 %copy.52 = bf16[15,1,4,256,256]{4,3,2,0,1:T(8,128)(2,1)} copy(bf16[15,1,4,256,256]{4,3,0,1,2:T(8,128)(2,1)} %bitcast.265) | data formatting | bytes 15728640 | tf_op jit(solution)/shard_map/reshape | solution.py:15
  293.1 10.8 %convolution_convert_fusion = bf16[15,256,1024]{2,1,0:T(8,128)(2,1)S(1)} fusion(bf16[15,1024,256]{2,1,0:T(8,128)(2,1)} %bitcast.272, bf16[1024,1024,1]{1,0,2:T(8,128)(2,1)S(1)} %copy-done.10), kind=kOutput, calls=%fused_computation.4 | convolution fusion | flops 8056995840 | bytes 17825792 | tf_op jit(solution)/shard_map/wz,fyzx->fywx/dot_general | solution.py:116
  303.9 2.7 slice_convert_fusion.3
  306.6 2.6 collective-permute-start.5
  309.3 34.1 %collective-permute-done.4 = bf16[3,1,1024,256]{2,3,1,0:T(8,128)(2,1)S(1)} collective-permute-done((bf16[3,1,1024,256]{2,3,1,0:T(8,128)(2,1)S(1)}, bf16[3,1,1024,256]{2,3,1,0:T(8,128)(2,1)S(1)}, u32[]{:S(2)}, u32[]{:S(2)}) %collective-permute-start.4) | collective-permute-done | bytes 1572896 | tf_op jit(solution)/shard_map/ppermute | solution.py:37
  345.1 3.3 collective-permute-start.7
  348.4 2.6 copy.66
  351.0 4.0 %pad_maximum_fusion.1 = bf16[3,3,1024,258]{2,3,1,0:T(8,128)(2,1)S(1)} fusion(bf16[3,3,1024,1]{2,3,1,0:T(2,128)(2,1)S(1)} %collective-permute-done.7, bf16[3,1,1024,256]{2,3,1,0:T(8,128)(2,1)} %copy-done.9, bf16[3,1,1024,256]{2,3,1,0:T(8,128)(2,1)} %copy-done.3, bf16[3,1,1024,256]{2,3,1,0:T(8,128)(2,1)} %copy-done.8, ...), kind=kLoop, calls=%fused_computation.5 | loop fusion | flops 23777280 | bytes 9510912 | tf_op jit(solution)/shard_map/concatenate | solution.py:39
  356.2 3.9 fusion.84
  360.1 3.3 fusion.4
  363.4 4.0 %fusion.13 = f32[3,1,1024,256]{2,3,1,0:T(8,128)S(1)} fusion(f32[3,1,1,256]{2,3,1,0:T(8,128)S(1)} %get-tuple-element.30, f32[3,1,1023,256]{2,3,1,0:T(8,128)} %get-tuple-element.16, f32[3,1,1023,256]{2,3,1,0:T(8,128)} %get-tuple-element.15, f32[3,1,1,256]{2,3,1,0:T(8,128)S(1)} %get-tuple-element.29), kind=kLoop, calls=%fused_computation.26 | loop fusion | flops 3145728 | bytes 9437184 | tf_op jit(solution)/shard_map/mul | solution.py:73
  367.4 4.5 %fusion.34 = (f32[]{:T(128)}, f32[1,1024,256]{1,2,0:T(8,128)S(1)}, f32[1,1024,256]{1,2,0:T(8,128)S(1)}, f32[1,1024,256]{1,2,0:T(8,128)S(1)}, f32[1,1024,256]{1,2,0:T(8,128)S(1)}) fusion(f32[3,1,1024,256]{2,3,1,0:T(8,128)S(1)} %copy-done.4, bf16[15,1,1024,256]{2,3,1,0:T(8,128)(2,1)} %bitcast.267, f32[3,1,1024,256]{2,3,1,0:T(8,128)S(1)} %get-tuple-element.17, ...), kind=kLoop, calls=%fused_computation.71 | loop fusion | flops 15204351 | bytes 16777220 | tf_op jit(solution)/shard_map/reduce_sum | solution.py:101
  372.0 2.7 fusion.55
  374.7 12.2 %all-reduce = (f32[1]{0:T(128)}, f32[1]{0:T(128)}) all-reduce(f32[1]{0:T(128)} %bitcast.59, f32[1]{0:T(128)} %bitcast.60), channel_id=1, replica_groups=mesh['py'=8,'pz'=4] {'pz'}, use_global_device_ids=true, to_apply=%region_1.2 | all-reduce | flops 2 | bytes 16 | tf_op jit(solution)/shard_map/psum | solution.py:121
  388.1 4.9 %fusion.40 = f32[1,256,1024]{2,1,0:T(8,128)} fusion(f32[]{:T(128)} %bitcast.61, f32[3,1,256,1024]{3,2,1,0:T(8,128)} %fusion.12, f32[3,1,256,1024]{3,2,1,0:T(8,128)} %copy-done.1, f32[3,1,256,1024]{3,2,1,0:T(8,128)S(1)} %get-tuple-element.19), kind=kLoop, calls=%fused_computation.77 | loop fusion | flops 6553600 | bytes 10485764 | tf_op jit(solution)/shard_map/mul | solution.py:124
  (62 shorter events, 28.2 us)
Async XLA Ops:
  0.6 9.0 %copy-start = (f32[3,1,256,1024]{3,2,1,0:T(8,128)S(1)}, f32[3,1,256,1024]{3,2,1,0:T(8,128)}, u32[]{:S(2)}) copy-start(f32[3,1,256,1024]{3,2,1,0:T(8,128)} %param.3) | copy-start | bytes 9437188
  0.6 69.7 %collective-permute-start = (f32[3,1,256,1024]{3,2,1,0:T(8,128)}, f32[3,1,256,1024]{3,2,1,0:T(8,128)S(1)}, u32[]{:S(2)}, u32[]{:S(2)}) collective-permute-start(f32[3,1,256,1024]{3,2,1,0:T(8,128)} %param.3), channel_id=1, source_target_pairs={{0,4},{4,8},{8,12},{12,16},{16,20},{20,24},{24,28},{28,0},{1,5},{5... | collective-permute-start | bytes 9437192 | tf_op jit(solution)/shard_map/ppermute | solution.py:37
  1.2 70.7 %collective-permute-start.1 = (f32[3,1,256,1024]{3,2,1,0:T(8,128)}, f32[3,1,256,1024]{3,2,1,0:T(8,128)S(1)}, u32[]{:S(2)}, u32[]{:S(2)}) collective-permute-start(f32[3,1,256,1024]{3,2,1,0:T(8,128)} %param.3), channel_id=1, source_target_pairs={{4,0},{8,4},{12,8},{16,12},{20,16},{24,20},{28,24},{0,28},{5,1},{9... | collective-permute-start | bytes 9437192 | tf_op jit(solution)/shard_map/ppermute | solution.py:38
  72.1 3.7 copy-start.5
  75.8 6.9 %collective-permute-start.2 = (f32[3,3,1,1024]{3,2,1,0:T(1,128)S(1)}, f32[3,3,1,1024]{3,2,1,0:T(1,128)S(1)}, u32[]{:S(2)}, u32[]{:S(2)}) collective-permute-start(f32[3,3,1,1024]{3,2,1,0:T(1,128)S(1)} %get-tuple-element.21), channel_id=1, source_target_pairs={{0,1},{1,2},{2,3},{3,0},{4,5},{5,6},{6,7},{7,4},{8,9},{9,10},{10,1... | collective-permute-start | bytes 110600 | tf_op jit(solution)/shard_map/ppermute | solution.py:37
  77.9 5.1 %collective-permute-start.3 = (f32[3,3,1,1024]{3,2,1,0:T(1,128)S(1)}, f32[3,3,1,1024]{3,2,1,0:T(1,128)S(1)}, u32[]{:S(2)}, u32[]{:S(2)}) collective-permute-start(f32[3,3,1,1024]{3,2,1,0:T(1,128)S(1)} %get-tuple-element.22), channel_id=1, source_target_pairs={{1,0},{2,1},{3,2},{0,3},{5,4},{6,5},{7,6},{4,7},{9,8},{10,9},{11,1... | collective-permute-start | bytes 110600 | tf_op jit(solution)/shard_map/ppermute | solution.py:38
  82.8 5.9 %copy-start.2 = (f32[3,1,256,1024]{3,2,1,0:T(8,128)S(1)}, f32[3,1,256,1024]{3,2,1,0:T(8,128)}, u32[]{:S(2)}) copy-start(f32[3,1,256,1024]{3,2,1,0:T(8,128)} %fusion.12) | copy-start | bytes 9437188
  88.7 6.3 %copy-start.1 = (f32[3,1,256,1024]{3,2,1,0:T(8,128)}, f32[3,1,256,1024]{3,2,1,0:T(8,128)S(1)}, u32[]{:S(2)}) copy-start(f32[3,1,256,1024]{3,2,1,0:T(8,128)S(1)} %get-tuple-element.20) | copy-start | bytes 9437188
  93.9 2.3 copy-start.10
  303.9 39.6 %copy-start.7 = (bf16[15,256,1024]{2,1,0:T(8,128)(2,1)}, bf16[15,256,1024]{2,1,0:T(8,128)(2,1)S(1)}, u32[]{:S(2)}) copy-start(bf16[15,256,1024]{2,1,0:T(8,128)(2,1)S(1)} %convolution_convert_fusion) | copy-start | bytes 23592964
  306.6 36.8 %copy-start.3 = (bf16[3,1,1024,256]{2,3,1,0:T(8,128)(2,1)}, bf16[3,1,1024,256]{2,3,1,0:T(8,128)(2,1)S(1)}, u32[]{:S(2)}) copy-start(bf16[3,1,1024,256]{2,3,1,0:T(8,128)(2,1)S(1)} %get-tuple-element.24) | copy-start | bytes 4718596
  306.6 36.8 %collective-permute-start.4 = (bf16[3,1,1024,256]{2,3,1,0:T(8,128)(2,1)S(1)}, bf16[3,1,1024,256]{2,3,1,0:T(8,128)(2,1)S(1)}, u32[]{:S(2)}, u32[]{:S(2)}) collective-permute-start(bf16[3,1,1024,256]{2,3,1,0:T(8,128)(2,1)S(1)} %get-tuple-element.24), channel_id=1, source_target_pairs={{0,4},{4,8},{8,12},{12,16},{16,20},{20,24},{24,28},{28,0},{1,5},{5... | collective-permute-start | bytes 4718600 | tf_op jit(solution)/shard_map/ppermute | solution.py:37
  306.6 36.8 %collective-permute-start.5 = (bf16[3,1,1024,256]{2,3,1,0:T(8,128)(2,1)S(1)}, bf16[3,1,1024,256]{2,3,1,0:T(8,128)(2,1)S(1)}, u32[]{:S(2)}, u32[]{:S(2)}) collective-permute-start(bf16[3,1,1024,256]{2,3,1,0:T(8,128)(2,1)S(1)} %get-tuple-element.24), channel_id=1, source_target_pairs={{4,0},{8,4},{12,8},{16,12},{20,16},{24,20},{28,24},{0,28},{5,1},{9... | collective-permute-start | bytes 4718600 | tf_op jit(solution)/shard_map/ppermute | solution.py:38
  343.4 1.2 copy-start.8
  343.4 1.6 copy-start.9
  344.6 6.4 %collective-permute-start.6 = (bf16[3,3,1024,1]{2,3,1,0:T(2,128)(2,1)S(1)}, bf16[3,3,1024,1]{2,3,1,0:T(2,128)(2,1)S(1)}, u32[]{:S(2)}, u32[]{:S(2)}) collective-permute-start(bf16[3,3,1024,1]{2,3,1,0:T(2,128)(2,1)S(1)} %get-tuple-element.34), channel_id=1, source_target_pairs={{0,1},{1,2},{2,3},{3,0},{4,5},{5,6},{6,7},{7,4},{8,9},{9,10},{10,1... | collective-permute-start | bytes 55304 | tf_op jit(solution)/shard_map/ppermute | solution.py:37
  345.1 5.9 %collective-permute-start.7 = (bf16[3,3,1024,1]{2,3,1,0:T(2,128)(2,1)S(1)}, bf16[3,3,1024,1]{2,3,1,0:T(2,128)(2,1)S(1)}, u32[]{:S(2)}, u32[]{:S(2)}) collective-permute-start(bf16[3,3,1024,1]{2,3,1,0:T(2,128)(2,1)S(1)} %get-tuple-element.35), channel_id=1, source_target_pairs={{1,0},{2,1},{3,2},{0,3},{5,4},{6,5},{7,6},{4,7},{9,8},{10,9},{11,1... | collective-permute-start | bytes 55304 | tf_op jit(solution)/shard_map/ppermute | solution.py:38
  363.4 4.0 %copy-start.4 = (f32[3,1,1024,256]{2,3,1,0:T(8,128)S(1)}, f32[3,1,1024,256]{2,3,1,0:T(8,128)}, u32[]{:S(2)}) copy-start(f32[3,1,1024,256]{2,3,1,0:T(8,128)} %get-tuple-element.18) | copy-start | bytes 9437188
  363.4 8.5 %slice-start = ((s8[7864320]{0:T(1024)(128)(4,1)}), s8[4194304]{0:T(1024)(128)(4,1)S(1)}, s32[]{:S(2)}) async-start(s8[7864320]{0:T(1024)(128)(4,1)} %bitcast.269), calls=%async_computation.1 | async-start | bytes 8388608
  367.4 4.5 %copy-start.6 = (f32[3,1,1024,256]{2,3,1,0:T(8,128)S(1)}, f32[3,1,1024,256]{2,3,1,0:T(8,128)}, u32[]{:S(2)}) copy-start(f32[3,1,1024,256]{2,3,1,0:T(8,128)} %get-tuple-element.23) | copy-start | bytes 9437188
  367.4 4.5 %slice-start.1 = ((s8[7864320]{0:T(1024)(128)(4,1)}), s8[3670016]{0:T(1024)(128)(4,1)S(1)}, s32[]{:S(2)}) async-start(s8[7864320]{0:T(1024)(128)(4,1)} %bitcast.269), calls=%async_computation.2 | async-start | bytes 7340032
